TPU v7x, 32 devices: a whole 2x2x4 slice. The times are simulated.
32 devices in a mesh: tm: 2 (over x), py: 4 (over z), pz: 4 (over y, core).
Axes of the slice: x: 2, y: 2, z: 4, core: 2. Of those that a mesh axis runs over, the one named last changes fastest.
Arguments:
- state_old: float32 [2, 4, 128, 128, 128], P('tm', None, 'py', 'pz'), may hold values from -6 to 6
Outputs:
- new_states: float32 [2, 4, 128, 128, 128], P('tm', None, 'py', 'pz')
All inputs are finite; a program needn't handle non-finite values.
Results may differ from a plain program's by a relative error of at most 0.00017.
Values sent between devices are 32-bit elements; how exact they have to be, the bound alone decides.
No kernel may reach another device: no remote copies, remote signals or barrier semaphores. Data moves between devices by JAX's collectives and lax.ppermute only.
A program may use at most 128 MiB of HBM per device.

v0:
```python
import jax
import jax.numpy as jnp
from jax import lax
from jax.sharding import PartitionSpec as P

KMAX = 42
KCO = 21


time_step = 0.01
coriolis = 6.0
buoyancy_square = 100.0
viscosity = 0.001
diffusivity = 0.001


def passed_along(value, axis, by):
    length = lax.axis_size(axis)
    pairs = [(i, i + by) for i in range(length) if 0 <= i + by < length]
    return lax.ppermute(value, axis, pairs)


def product(form, left, right):
    return jnp.einsum(
        form, left, right, precision=lax.Precision.HIGHEST, preferred_element_type=jnp.float32
    )


def radians(waves, extent):
    cells = jnp.arange(extent)
    return 2.0 * jnp.pi / extent * (waves[:, None] * cells[None, :] % extent).astype(jnp.float32)


def first_tables(slots, extent):
    waves = jnp.arange(slots)
    inside = (waves <= KMAX).astype(jnp.float32)[:, None]
    angle = radians(waves, extent)
    scale = extent ** (-0.5)
    forward = jnp.stack([jnp.cos(angle), -jnp.sin(angle)]) * (inside * scale)
    weight = jnp.where(waves == 0, 1.0, 2.0).astype(jnp.float32)[:, None] * inside * scale
    backward = jnp.stack([jnp.cos(angle), -jnp.sin(angle)]) * weight
    return (forward, backward)


def complex_block(real_part, imag_part):
    upper = jnp.stack([real_part, imag_part], axis=1)
    lower = jnp.stack([-imag_part, real_part], axis=1)
    return jnp.stack([upper, lower])


def other_tables(slots, extent):
    waves = jnp.arange(slots) - KMAX
    inside = (waves <= KMAX).astype(jnp.float32)[:, None]
    angle = radians(waves, extent)
    scale = extent ** (-0.5)
    cosine = jnp.cos(angle) * inside * scale
    sine = jnp.sin(angle) * inside * scale
    return (complex_block(cosine.T, -sine.T), complex_block(cosine, sine))


def wave_parts(first_index, second_index, third_slots):
    wave_x = first_index.astype(jnp.float32)[:, None, None]
    wave_y = (second_index - KMAX).astype(jnp.float32)[None, :, None]
    third = (third_slots - KMAX).astype(jnp.float32)
    third = jnp.concatenate([third, third])
    return (wave_x, wave_y, third[None, None, :])


def coarse_inside(waves):
    wave_x, wave_y, wave_z = waves
    return (wave_x <= KCO) & (jnp.abs(wave_y) <= KCO) & (jnp.abs(wave_z) <= KCO)


def times_i(values):
    half = values.shape[-1] // 2
    return jnp.concatenate([-values[..., half:], values[..., :half]], axis=-1)


def squared(waves):
    wave_x, wave_y, wave_z = waves
    return wave_x**2 + wave_y**2 + wave_z**2


def project(velocity, waves):
    wave_x, wave_y, wave_z = waves
    along = (wave_x * velocity[0] + wave_y * velocity[1] + wave_z * velocity[2]) / jnp.maximum(
        squared(waves), 1.0
    )
    return (
        velocity[0] - wave_x * along,
        velocity[1] - wave_y * along,
        velocity[2] - wave_z * along,
    )


def linear(state, waves):
    square = squared(waves)
    pushed = project((coriolis * state[1], -coriolis * state[0], state[3]), waves)
    return jnp.stack(
        [
            pushed[0] - viscosity * square * state[0],
            pushed[1] - viscosity * square * state[1],
            pushed[2] - viscosity * square * state[2],
            -buoyancy_square * state[2] - diffusivity * square * state[3],
        ]
    )


def propagate(state, waves):
    for half_step in range(2):
        anchor = state
        for order in (4.0, 3.0, 2.0, 1.0):
            state = anchor + 0.5 * time_step / order * linear(state, waves)
    return state


def rate(state, waves, to_grid, to_modes):
    wave_x, wave_y, wave_z = waves
    square = squared(waves)
    spin = jnp.stack(
        [
            times_i(wave_y * state[2] - wave_z * state[1]),
            times_i(wave_z * state[0] - wave_x * state[2]),
            times_i(wave_x * state[1] - wave_y * state[0]),
        ]
    )
    fields = to_grid(jnp.concatenate([state, spin]))
    speed_x, speed_y, speed_z, lift = (fields[0], fields[1], fields[2], fields[3])
    spin_x, spin_y, spin_z = (fields[4], fields[5], fields[6])
    products = jnp.stack(
        [
            speed_y * spin_z - speed_z * spin_y,
            speed_z * spin_x - speed_x * spin_z,
            speed_x * spin_y - speed_y * spin_x,
            speed_x * lift,
            speed_y * lift,
            speed_z * lift,
        ]
    )
    modes = to_modes(products)
    pushed = project(
        (modes[0] + coriolis * state[1], modes[1] - coriolis * state[0], modes[2] + state[3]), waves
    )
    lift_rate = (
        -times_i(wave_x * modes[3] + wave_y * modes[4] + wave_z * modes[5])
        - buoyancy_square * state[2]
        - diffusivity * square * state[3]
    )
    return jnp.stack(
        [
            pushed[0] - viscosity * square * state[0],
            pushed[1] - viscosity * square * state[1],
            pushed[2] - viscosity * square * state[2],
            lift_rate,
        ]
    )


def on_device(state_old):
    fields_grid = state_old[0]
    extent = fields_grid.shape[-1]
    rows_y, rows_z = (fields_grid.shape[1], fields_grid.shape[2])
    across_y = lax.axis_size("py")
    across_z = lax.axis_size("pz")
    joint = across_y * across_z
    first_slots = (KMAX + joint) // joint * joint
    other_slots = (2 * KMAX + across_z) // across_z * across_z
    fore_first, back_first = first_tables(first_slots, extent)
    fore_other, back_other = other_tables(other_slots, extent)
    width_x = first_slots // joint
    first_index = lax.axis_index(("py", "pz")) * width_x + jnp.arange(width_x)
    second_index = jnp.arange(other_slots)
    fore_y_blocks = fore_other.reshape(2, across_y, rows_y, 2, other_slots)
    fore_z_blocks = fore_other.reshape(2, across_z, rows_z, 2, other_slots)
    back_y_blocks = back_other.reshape(2, other_slots, 2, across_y, rows_y)

    def to_modes(physical):
        spread = product("fyzx,cax->fcayz", physical, fore_first)[None]

        def last_step(arrived):
            count = arrived.shape[1]
            blocks = arrived.reshape(across_y, across_z, count, 2, width_x, rows_y, rows_z)
            along_y = product("jkfcayz,cjyeb->kfeabz", blocks, fore_y_blocks)
            along_z = product("kfeabz,ekzgd->fabgd", along_y, fore_z_blocks)
            return along_z.reshape(count, width_x, other_slots, 2 * other_slots)

        return last_step(
            lax.all_to_all(spread, ("py", "pz"), split_axis=3, concat_axis=0, tiled=True)
        )

    def to_grid(modes):
        count = modes.shape[0]
        view = modes.reshape(count, width_x, other_slots, 2, other_slots)
        along_z = product("fabck,ckez->feabz", view, back_other)
        along_z = along_z.reshape(count, 2, width_x, other_slots, across_z, rows_z)
        blocks = product("feabkm,ebgjl->jkfgalm", along_z, back_y_blocks)
        blocks = blocks.reshape(joint, count, 2, width_x, rows_y, rows_z)

        def last_step(received):
            return product("ofcayz,cax->fyzx", received, back_first)

        return last_step(
            lax.all_to_all(blocks, ("py", "pz"), split_axis=0, concat_axis=3, tiled=True)
        )

    waves = wave_parts(first_index, second_index, jnp.arange(other_slots))
    start = to_modes(fields_grid)
    velocity = project((start[0], start[1], start[2]), waves)
    start = jnp.concatenate([jnp.stack(velocity), start[3:]])
    fine = start + time_step * rate(start, waves, to_grid, to_modes)
    band_slots = jnp.arange(other_slots)
    chain_waves = wave_parts(first_index, second_index, band_slots)
    keep = coarse_inside(chain_waves).astype(jnp.float32)
    later_slice = lax.axis_index("tm") > 0
    local = keep * fine - jnp.where(later_slice, keep * propagate(start, chain_waves), 0.0)

    def relay(turn, carry):
        arrived = passed_along(carry, "tm", 1)
        return local + keep * propagate(arrived, chain_waves)

    carry = lax.fori_loop(0, lax.axis_size("tm") - 1, relay, local)
    merged = jnp.where(coarse_inside(waves), carry, fine)
    return to_grid(merged)[None]


def solution(mesh):
    return jax.shard_map(
        on_device,
        mesh=mesh,
        in_specs=(P("tm", None, "py", "pz", None),),
        out_specs=P("tm", None, "py", "pz", None),
        check_vma=False,
    )
```

profile of v0, /device:TPU:11, one launch (start us, length us, event | category | flops | bytes accessed | tf_op | source)
XLA Modules:
  0.0 502.6 jit_solution(3868148268568949657)
XLA Ops:
  0.2 0.6 copy-done.12
  0.7 0.9 copy-done
  1.6 5.2 %convolution_bitcast_fusion.2 = f32[1,4,2,48,32,32]{3,5,4,1,2,0:T(8,128)} fusion(f32[1,4,32,32,128]{4,3,2,1,0:T(8,128)S(1)} %copy-done, f32[48]{0:T(128)S(1)} %compare_select_fusion.2, f32[1,48,128]{2,1,0:T(8,128)S(1)} %get-tuple-element.155, f32[1,48,128]{2,1,0:T(8,128)S(1)} %get-tuple-element.156), kind=kOutput, calls=%fused_computation.15 | convolution fusion | flops 604004352 | bytes 3719360 | tf_op jit(solution)/shard_map/fyzx,cax->fcayz/dot_general | solution.py:24
  6.8 7.7 %copy.68 = f32[1,4,2,48,32,32]{5,4,1,2,0,3:T(8,128)} copy(f32[1,4,2,48,32,32]{3,5,4,1,2,0:T(8,128)} %convolution_bitcast_fusion.2) | data formatting | bytes 3145728 | tf_op jit(solution)/shard_map/broadcast_in_dim | solution.py:178
  14.6 5.9 %reshape.1277 = f32[16,1,24576]{2,1,0:T(1,128)} reshape(f32[48,1,2,4,32,32]{5,4,3,2,1,0:T(8,128)} %bitcast.287) | data formatting | bytes 3145728
  20.5 6.6 %all-to-all-start = ((f32[16,1,24576]{2,1,0:T(1,128)}), f32[16,1,24576]{2,1,0:T(1,128)S(1)}, u32[]{:S(2)}, u32[]{:S(2)}) async-start(f32[16,1,24576]{2,1,0:T(1,128)} %reshape.1277), calls=%async_computation | async-start | bytes 3145728 | tf_op jit(solution)/shard_map/all_to_all | solution.py:188
  27.1 0.7 pad_maximum_fusion.9
  28.8 0.7 maximum_bitcast_fusion.3
  29.9 1.0 multiply_multiply_fusion.2
  30.9 31.7 %all-to-all-done = f32[16,1,24576]{2,1,0:T(1,128)S(1)} async-done(((f32[16,1,24576]{2,1,0:T(1,128)}), f32[16,1,24576]{2,1,0:T(1,128)S(1)}, u32[]{:S(2)}, u32[]{:S(2)}) %all-to-all-start) | async-done | bytes 1572896 | tf_op jit(solution)/shard_map/all_to_all | solution.py:188
  62.6 0.6 broadcast.2363
  63.2 4.4 reduce.4
  67.6 4.0 reshape.1278
  71.5 3.5 copy.69
  75.0 10.2 %fusion.4 = f32[2,88,4,4,3,32,1,1]{1,5,7,6,2,0,4,3:T(8,128)S(1)} fusion(f32[4,4,4,2,3,32,32,1]{6,5,4,1,0,3,2,7:T(8,128)S(1)} %bitcast.286, f32[1,4,32,1,88]{4,2,1,0,3:T(8,128)S(1)} %get-tuple-element.147, f32[1,4,32,1,88]{4,2,1,0,3:T(8,128)S(1)} %get-tuple-element.146, f32[1,4,32,1,88]{4,2,1,0,3:T(8,128)S(1)} %get-tuple-element.145), kind=kOutput, calls=%fused_computation.4 | convolution fusion | flops 830607360 | bytes 2789376 | tf_op jit(solution)/shard_map/jkfcayz,cjyeb->kfeabz/dot_general | solution.py:24
  85.3 2.7 fusion.32
  88.0 0.9 subtract_dynamic-update-slice_fusion.5
  88.9 1.5 fusion.281
  92.3 0.7 subtract_dynamic-update-slice_fusion.3
  93.1 0.7 constant_dynamic-update-slice_fusion.3
  93.8 0.7 constant_dynamic-update-slice_fusion.2
  94.5 0.7 constant_dynamic-update-slice_fusion.1
  95.2 0.7 constant_dynamic-update-slice_fusion
  96.0 3.8 fusion.24
  99.8 2.2 copy.82
  102.0 10.5 %convolution_bitcast_fusion = f32[4,4,7,2,3,32,32]{6,5,1,4,2,0,3:T(8,128)S(1)} fusion(f32[7,2,3,88,4,32,1,1]{3,5,4,2,1,0,7,6:T(8,128)} %bitcast.291, f32[1,88,1,4,32]{1,4,0,3,2:T(8,128)S(1)} %copy-done.22, f32[1,88,1,4,32]{1,4,0,3,2:T(8,128)S(1)} %copy-done.20, f32[1,88,1,4,32]{1,4,0,3,2:T(8,128)S(1)} %copy-done.18), kind=kOutput, calls=%fused_computation.8 | convolution fusion | flops 1453461504 | bytes 4780032 | tf_op jit(solution)/shard_map/feabkm,ebgjl->jkfgalm/dot_general | solution.py:24
  112.5 6.1 %copy.84 = f32[4,4,7,2,3,32,32]{6,5,4,3,2,1,0:T(8,128)} copy(f32[4,4,7,2,3,32,32]{6,5,1,4,2,0,3:T(8,128)S(1)} %convolution_bitcast_fusion) | data formatting | bytes 5505024 | tf_op jit(solution)/shard_map/feabkm,ebgjl->jkfgalm/transpose | solution.py:24
  118.6 9.8 %reshape.1279 = f32[16,1,43008]{2,1,0:T(1,128)} reshape(f32[16,7,2,3,32,32]{5,4,3,2,1,0:T(8,128)} %bitcast.279) | data formatting | bytes 5505024
  128.4 5.7 %all-to-all-start.1 = ((f32[16,1,43008]{2,1,0:T(1,128)}), f32[16,1,43008]{2,1,0:T(1,128)S(1)}, u32[]{:S(2)}, u32[]{:S(2)}) async-start(f32[16,1,43008]{2,1,0:T(1,128)} %reshape.1279), calls=%async_computation.1 | async-start | bytes 5505024 | tf_op jit(solution)/shard_map/all_to_all | solution.py:203
  134.1 59.2 %all-to-all-done.1 = f32[16,1,43008]{2,1,0:T(1,128)S(1)} async-done(((f32[16,1,43008]{2,1,0:T(1,128)}), f32[16,1,43008]{2,1,0:T(1,128)S(1)}, u32[]{:S(2)}, u32[]{:S(2)}) %all-to-all-start.1) | async-done | bytes 2752544 | tf_op jit(solution)/shard_map/all_to_all | solution.py:203
  193.3 9.6 %reduce.5 = f32[16,43008]{1,0:T(8,128)} reduce(f32[16,1,43008]{2,1,0:T(1,128)S(1)} %all-to-all-done.1, f32[]{:T(128)} %broadcast.2363), dimensions={1}, to_apply=%all_to_all.47.reduce_sub_computation | reduce | bytes 5505028 | tf_op jit(solution)/shard_map/all_to_all | solution.py:203
  202.9 11.3 %reshape.1280 = f32[16,7,2,3,32,32]{5,4,3,2,1,0:T(8,128)} reshape(f32[16,43008]{1,0:T(8,128)} %reduce.5) | data formatting | bytes 5505024
  214.2 6.1 %copy.85 = f32[1,7,2,16,3,32,32]{6,5,4,3,2,1,0:T(8,128)S(1)} copy(f32[1,7,2,16,3,32,32]{6,5,4,2,1,3,0:T(8,128)} %bitcast.280) | data formatting | bytes 5505024 | tf_op jit(solution)/shard_map/all_to_all | solution.py:203
  220.3 21.6 %fusion.16 = f32[7,32,32,128]{3,2,1,0:T(8,128)S(1)} fusion(f32[7,2,48,32,32]{4,3,2,1,0:T(8,128)S(1)} %bitcast.281, f32[48]{0:T(128)S(1)} %fusion.246, f32[1,48,128]{2,1,0:T(8,128)S(1)} %copy-done.13, f32[1,48,128]{2,1,0:T(8,128)S(1)} %copy-done.16), kind=kOutput, calls=%fused_computation.17 | convolution fusion | flops 1056989184 | bytes 6471872 | tf_op jit(solution)/shard_map/ofcayz,cax->fyzx/dot_general | solution.py:24
  242.8 0.5 copy-done.34
  243.4 7.1 %fusion.10 = f32[1,6,2,48,32,32]{3,5,4,1,2,0:T(8,128)} fusion(f32[6,32,32,128]{3,2,1,0:T(8,128)S(1)} %multiply_dynamic-update-slice_fusion, f32[48]{0:T(128)S(1)} %copy-done.34, f32[1,48,128]{2,1,0:T(8,128)S(1)} %copy-done.13, f32[1,48,128]{2,1,0:T(8,128)S(1)} %copy-done.16), kind=kOutput, calls=%fused_computation.12 | convolution fusion | flops 905994240 | bytes 5554368 | tf_op jit(solution)/shard_map/fyzx,cax->fcayz/dot_general | solution.py:24
  250.5 10.9 %copy.87 = f32[1,6,2,48,32,32]{5,4,1,2,0,3:T(8,128)} copy(f32[1,6,2,48,32,32]{3,5,4,1,2,0:T(8,128)} %fusion.10) | data formatting | bytes 4718592 | tf_op jit(solution)/shard_map/broadcast_in_dim | solution.py:178
  261.4 9.1 %reshape.1281 = f32[16,1,36864]{2,1,0:T(1,128)} reshape(f32[48,1,2,6,32,32]{5,4,3,2,1,0:T(8,128)} %bitcast.282) | data formatting | bytes 4718592
  270.5 6.9 %all-to-all-start.2 = ((f32[16,1,36864]{2,1,0:T(1,128)}), f32[16,1,36864]{2,1,0:T(1,128)S(1)}, u32[]{:S(2)}, u32[]{:S(2)}) async-start(f32[16,1,36864]{2,1,0:T(1,128)} %reshape.1281), calls=%async_computation.2 | async-start | bytes 4718592 | tf_op jit(solution)/shard_map/all_to_all | solution.py:188
  277.6 0.8 broadcast_and_fusion
  278.4 1.1 copy.75
  279.5 49.2 %all-to-all-done.2 = f32[16,1,36864]{2,1,0:T(1,128)S(1)} async-done(((f32[16,1,36864]{2,1,0:T(1,128)}), f32[16,1,36864]{2,1,0:T(1,128)S(1)}, u32[]{:S(2)}, u32[]{:S(2)}) %all-to-all-start.2) | async-done | bytes 2359328 | tf_op jit(solution)/shard_map/all_to_all | solution.py:188
  328.8 8.5 %reduce.6 = f32[16,36864]{1,0:T(8,128)} reduce(f32[16,1,36864]{2,1,0:T(1,128)S(1)} %all-to-all-done.2, f32[]{:T(128)} %broadcast.2363), dimensions={1}, to_apply=%all_to_all.50.reduce_sub_computation | reduce | bytes 4718596 | tf_op jit(solution)/shard_map/all_to_all | solution.py:188
  337.3 10.2 %reshape.1282 = f32[48,1,2,6,32,32]{5,4,3,2,1,0:T(8,128)} reshape(f32[16,36864]{1,0:T(8,128)} %reduce.6) | data formatting | bytes 4718592
  347.5 4.8 copy.88
  352.4 15.7 %fusion.2 = f32[2,88,4,6,3,32,1,1]{1,5,7,6,2,0,4,3:T(8,128)S(1)} fusion(f32[4,4,6,2,3,32,32,1]{6,5,4,1,0,3,2,7:T(8,128)S(1)} %bitcast.284, f32[1,4,32,1,88]{4,2,1,0,3:T(8,128)S(1)} %copy-done.6, f32[1,4,32,1,88]{4,2,1,0,3:T(8,128)S(1)} %get-tuple-element.146, f32[1,4,32,1,88]{4,2,1,0,3:T(8,128)S(1)} %get-tuple-element.145), kind=kOutput, calls=%fused_computation.2 | convolution fusion | flops 1245843456 | bytes 4116480 | tf_op jit(solution)/shard_map/jkfcayz,cjyeb->kfeabz/dot_general | solution.py:24
  368.1 3.9 fusion.29
  373.2 0.6 copy-done.3
  374.3 0.5 subtract_subtract_fusion.2
  380.7 0.7 copy-done.4
  381.3 0.6 fusion.46
  381.9 1.5 collective-permute-start
  383.4 25.3 %collective-permute-done = f32[4,3,88,176]{2,3,1,0:T(8,128)S(1)} collective-permute-done((f32[4,3,88,176]{2,3,1,0:T(8,128)S(1)}, f32[4,3,88,176]{2,3,1,0:T(8,128)S(1)}, u32[]{:S(2)}, u32[]{:S(2)}) %collective-permute-start) | collective-permute-done | bytes 743456 | tf_op jit(solution)/shard_map/while/body/eval_jaxpr/ppermute | solution.py:20
  414.3 0.6 copy-done.24
  415.0 0.9 fusion.57
  416.0 2.3 convolution_bitcast_fusion.3
  419.1 5.2 %convolution_bitcast_fusion.1 = f32[4,4,4,2,3,32,32]{6,5,1,4,2,0,3:T(8,128)S(1)} fusion(f32[4,2,3,88,4,32,1,1]{3,5,4,2,1,0,7,6:T(8,128)S(1)} %bitcast.292, f32[1,88,1,4,32]{1,4,0,3,2:T(8,128)S(1)} %copy-done.23, f32[1,88,1,4,32]{1,4,0,3,2:T(8,128)S(1)} %copy-done.21, f32[1,88,1,4,32]{1,4,0,3,2:T(8,128)S(1)} %copy-done.19), kind=kOutput, calls=%fused_computation.11 | convolution fusion | flops 830607360 | bytes 2789376 | tf_op jit(solution)/shard_map/feabkm,ebgjl->jkfgalm/dot_general | solution.py:24
  424.3 3.3 copy.100
  427.7 5.0 reshape.1283
  432.7 44.3 %all_to_all.60 = f32[16,1,24576]{2,1,0:T(1,128)S(1)} all-to-all(f32[16,1,24576]{2,1,0:T(1,128)S(1)} %reshape.1283), channel_id=1, replica_groups=mesh['tm'=2,'py'=4,'pz'=4] {'py','pz'}, dimensions={0} | all-to-all | bytes 3145728 | tf_op jit(solution)/shard_map/all_to_all | solution.py:203
  477.0 4.4 reduce.7
  481.4 3.8 reshape.1284
  485.2 3.5 copy.101
  488.8 13.4 %fusion.21 = f32[1,4,32,32,128]{4,3,2,1,0:T(8,128)} fusion(f32[4,2,48,32,32]{4,3,2,1,0:T(8,128)S(1)} %bitcast.285, f32[48]{0:T(128)S(1)} %copy-done.36, f32[1,48,128]{2,1,0:T(8,128)S(1)} %copy-done.14, f32[1,48,128]{2,1,0:T(8,128)S(1)} %copy-done.17), kind=kOutput, calls=%fused_computation.20 | convolution fusion | flops 604004352 | bytes 3719360 | tf_op jit(solution)/shard_map/ofcayz,cax->fyzx/dot_general | solution.py:24
  (165 shorter events, 18.4 us)
Async XLA Ops:
  0.0 1.6 copy-start
  0.1 0.6 copy-start.12
  0.1 0.6 copy-start.15
  0.2 0.6 copy-start.33
  20.5 42.1 %all-to-all-start = ((f32[16,1,24576]{2,1,0:T(1,128)}), f32[16,1,24576]{2,1,0:T(1,128)S(1)}, u32[]{:S(2)}, u32[]{:S(2)}) async-start(f32[16,1,24576]{2,1,0:T(1,128)} %reshape.1277), calls=%async_computation | async-start | bytes 3145728 | tf_op jit(solution)/shard_map/all_to_all | solution.py:188
  27.1 60.9 %copy-start.25 = (f32[88]{0:T(128)}, f32[88]{0:T(128)S(1)}, u32[]{:S(2)}) copy-start(f32[88]{0:T(128)S(1)} %fusion.247) | copy-start | bytes 1060
  27.8 60.2 %copy-start.31 = (f32[2,88]{1,0:T(2,128)}, f32[2,88]{1,0:T(2,128)S(1)}, u32[]{:S(2)}) copy-start(f32[2,88]{1,0:T(2,128)S(1)} %mul.2992) | copy-start | bytes 2116
  28.0 60.0 %copy-start.27 = (f32[3]{0:T(128)}, f32[3]{0:T(128)S(1)}, u32[]{:S(2)}) copy-start(f32[3]{0:T(128)S(1)} %add_convert_fusion.1) | copy-start | bytes 40
  29.9 55.4 %copy-start.5 = (f32[1,4,32,1,88]{4,2,1,0,3:T(8,128)}, f32[1,4,32,1,88]{4,2,1,0,3:T(8,128)S(1)}, u32[]{:S(2)}) copy-start(f32[1,4,32,1,88]{4,2,1,0,3:T(8,128)S(1)} %get-tuple-element.147) | copy-start | bytes 135172
  90.3 0.7 copy-start.7
  90.3 0.7 copy-start.26
  90.3 0.7 copy-start.28
  90.7 0.7 copy-start.2
  91.7 0.7 copy-start.32
  93.1 2.9 copy-start.8
  93.1 2.9 copy-start.10
  99.8 2.2 copy-start.18
  99.8 2.2 copy-start.20
  99.8 2.2 copy-start.22
  128.4 64.9 %all-to-all-start.1 = ((f32[16,1,43008]{2,1,0:T(1,128)}), f32[16,1,43008]{2,1,0:T(1,128)S(1)}, u32[]{:S(2)}, u32[]{:S(2)}) async-start(f32[16,1,43008]{2,1,0:T(1,128)} %reshape.1279), calls=%async_computation.1 | async-start | bytes 5505024 | tf_op jit(solution)/shard_map/all_to_all | solution.py:203
  134.1 86.1 %copy-start.35 = (f32[48]{0:T(128)}, f32[48]{0:T(128)S(1)}, u32[]{:S(2)}) copy-start(f32[48]{0:T(128)S(1)} %fusion.246) | copy-start | bytes 580
  214.1 6.1 %copy-start.13 = (f32[1,48,128]{2,1,0:T(8,128)S(1)}, f32[1,48,128]{2,1,0:T(8,128)}, u32[]{:S(2)}) copy-start(f32[1,48,128]{2,1,0:T(8,128)} %copy-done.12) | copy-start | bytes 73732
  214.2 6.1 %copy-start.16 = (f32[1,48,128]{2,1,0:T(8,128)S(1)}, f32[1,48,128]{2,1,0:T(8,128)}, u32[]{:S(2)}) copy-start(f32[1,48,128]{2,1,0:T(8,128)} %copy-done.15) | copy-start | bytes 73732
  242.7 0.6 copy-start.34
  270.5 58.3 %all-to-all-start.2 = ((f32[16,1,36864]{2,1,0:T(1,128)}), f32[16,1,36864]{2,1,0:T(1,128)S(1)}, u32[]{:S(2)}, u32[]{:S(2)}) async-start(f32[16,1,36864]{2,1,0:T(1,128)} %reshape.1281), calls=%async_computation.2 | async-start | bytes 4718592 | tf_op jit(solution)/shard_map/all_to_all | solution.py:188
  347.5 4.8 copy-start.6
  372.4 0.7 copy-start.29
  372.8 1.0 copy-start.3
  373.8 0.6 copy-start.30
  380.4 1.0 copy-start.4
  381.9 26.8 %collective-permute-start = (f32[4,3,88,176]{2,3,1,0:T(8,128)S(1)}, f32[4,3,88,176]{2,3,1,0:T(8,128)S(1)}, u32[]{:S(2)}, u32[]{:S(2)}) collective-permute-start(f32[4,3,88,176]{2,3,1,0:T(8,128)S(1)} %fusion.46), channel_id=1, source_target_pairs={{0,16},{1,17},{2,18},{3,19},{4,20},{5,21},{6,22},{7,23},{8,24},{9,... | collective-permute-start | bytes 2230280 | tf_op jit(solution)/shard_map/while/body/eval_jaxpr/ppermute | solution.py:20
  414.1 0.9 copy-start.24
  415.0 1.0 copy-start.9
  415.0 1.0 copy-start.11
  418.2 0.8 copy-start.19
  418.2 0.9 copy-start.21
  418.3 0.9 copy-start.23
  485.2 3.5 copy-start.14
  485.2 3.5 copy-start.17
  485.2 3.5 copy-start.36
  488.8 13.4 %copy-start.1 = (f32[1,4,32,32,128]{4,3,2,1,0:T(8,128)S(1)}, f32[1,4,32,32,128]{4,3,2,1,0:T(8,128)}, u32[]{:S(2)}) copy-start(f32[1,4,32,32,128]{4,3,2,1,0:T(8,128)} %param.1) | copy-start | bytes 6291460
where the time goes:
time: 511 us; the launch traced here: 503 us
  waiting for transfers between devices  165 us (32%)
  local copies, waits for them, and re-layouts  119 us (23%)
  matrix products  102 us (20%)
  other arithmetic  49.8 us (10%)
  blocking collectives  44.3 us (9%)
  starting transfers between devices  20.6 us (4%)
    dot_general x12, matrix products, product(): jnp.einsum(form, left, right, precision=lax.Precision.HIGHEST, preferred_...  102 us
    all_to_all x2, waiting for transfers between devices, to_modes(): lax.all_to_all(spread, ('py', 'pz'), split_axis=3, concat_axis=0, tiled=T...  80.9 us
    unnamed x85, local copies, waits for them, and re-layouts  66.6 us
    all_to_all x1, waiting for transfers between devices, to_grid(): lax.all_to_all(blocks, ('py', 'pz'), split_axis=0, concat_axis=3, tiled=T...  59.2 us
    all_to_all x1, blocking collectives, to_grid(): lax.all_to_all(blocks, ('py', 'pz'), split_axis=0, concat_axis=3, tiled=T...  44.3 us
    ppermute x1, waiting for transfers between devices, passed_along(): return lax.ppermute(value, axis, pairs)  25.3 us
    broadcast_in_dim x2, local copies, waits for them, and re-layouts, to_modes(): spread = product('fyzx,cax->fcayz', physical, fore_first)[None]  18.7 us
    all_to_all x2, other arithmetic, to_grid(): lax.all_to_all(blocks, ('py', 'pz'), split_axis=0, concat_axis=3, tiled=T...  13.9 us
  transfers between devices with their start and end apart: 4, of which 4 were waited for; matrix products, arithmetic and copies ran while one was open for 1% of the time, Pallas kernels for 0%

commit v1 on v0

v1 whole, which is shorter than its diff:
```python
import functools

import jax
import jax.numpy as jnp
import numpy as np
from jax import lax
from jax.experimental import pallas as pl
from jax.experimental.pallas import tpu as pltpu
from jax.sharding import PartitionSpec as P

KMAX = 42
KCO = 21

time_step = 0.01
coriolis = 6.0
buoyancy_square = 100.0
viscosity = 0.001
diffusivity = 0.001

LANES = 128
PAIRS = ("py", "pz")
VMEM_LIMIT = 56 * 1024 * 1024


def up_to(value, step):
    return (value + step - 1) // step * step


class Plan:
    def __init__(self, shape, across_t, across_y, across_z):
        _, self.fields, self.rows_y, self.rows_z, self.extent = shape
        self.across_t, self.across_y, self.across_z = across_t, across_y, across_z
        self.joint = across_y * across_z
        self.slots = up_to(KMAX + 1, self.joint) // self.joint
        self.coarse_slots = up_to(KCO + 1, self.joint) // self.joint
        self.group = LANES // self.rows_z
        self.tiles = self.rows_y * self.rows_z // LANES
        self.waves = 2 * KMAX + 1
        self.wave_rows = up_to(self.waves, 8)
        self.coarse_rows = up_to(2 * KCO + 1, 8)
        assert self.extent == LANES and self.extent > 3 * KMAX
        assert self.group == self.across_z and self.tiles == 8
        assert 2 * KCO + 1 <= LANES // 2 <= self.waves <= LANES
        inner = list(range(-KCO, KCO + 1))
        outer = [k for k in range(-KMAX, KMAX + 1) if abs(k) > KCO]
        self.order = np.array(inner + outer)

    def angle(self, waves, cells):
        return 2.0 * np.pi / self.extent * ((waves[:, None] * cells[None, :]) % self.extent)

    def first(self):
        cells = np.arange(self.extent)
        waves = np.arange(self.slots * self.joint)
        inside = (waves <= KMAX)[:, None] * self.extent**-0.5
        weight = np.where(waves == 0, 1.0, 2.0)[:, None] * inside
        angle = self.angle(waves, cells)
        both = np.stack([np.cos(angle), -np.sin(angle)])

        def rows(table):
            table = table.reshape(2, self.slots, self.joint, self.extent)
            return table.transpose(1, 0, 2, 3).reshape(-1, self.extent)

        return rows(both * inside), rows(both * weight).T

    def other(self, size, cells):
        angle = self.angle(self.order, cells)
        cosine = np.zeros((size, len(cells)))
        sine = np.zeros((size, len(cells)))
        cosine[: self.waves] = np.cos(angle) * self.extent**-0.5
        sine[: self.waves] = np.sin(angle) * self.extent**-0.5
        return cosine, sine

    def along_z(self):
        cosine, sine = self.other(LANES, np.arange(self.extent))
        fore = np.block([[cosine.T, -sine.T], [sine.T, cosine.T]])
        back = np.block([[cosine, sine], [-sine, cosine]])
        return fore, back

    def along_y(self):
        cell = np.arange(self.extent).reshape(self.across_y, self.tiles, self.group)
        cosine, sine = self.other(self.wave_rows, cell.transpose(0, 2, 1).reshape(-1))
        fore = np.block([[cosine, sine], [-sine, cosine]])
        back = np.block([[cosine.T, -sine.T], [sine.T, cosine.T]])
        return fore, back

    def wave_tables(self):
        wave_y = np.zeros((self.wave_rows, LANES), np.float32)
        wave_y[: self.waves] = self.order[:, None]
        wave_z = np.zeros((self.wave_rows, LANES), np.float32)
        wave_z[:, : self.waves] = self.order[None, :]
        packed_z = np.tile(self.order[: LANES // 2], 2)
        packed_z = np.broadcast_to(packed_z, (self.coarse_rows, LANES))
        return wave_y, wave_z, packed_z.astype(np.float32)


def split_table(table):
    high = np.asarray(table, np.float32).astype(jnp.bfloat16)
    low = (table - high.astype(np.float64)).astype(np.float32).astype(jnp.bfloat16)
    return high, low


def split(values):
    high = values.astype(jnp.bfloat16)
    low = (values - high.astype(jnp.float32)).astype(jnp.bfloat16)
    return high, low


def dot(left, right, dims=((1,), (0,))):
    return lax.dot_general(left, right, (dims, ((), ())), preferred_element_type=jnp.float32)


def from_left(table, values, dims=((1,), (0,))):
    high, low = split(values)
    table_high, table_low = table[0][...], table[1][...]
    return dot(table_high, high, dims) + (dot(table_high, low, dims) + dot(table_low, high, dims))


def from_right(values, table):
    high, low = split(values)
    table_high, table_low = table[0][...], table[1][...]
    return dot(high, table_high) + (dot(low, table_high) + dot(high, table_low))


def swap_lanes(tiles, width):
    tiles = list(tiles)
    count = len(tiles)
    assert count * width == LANES
    lane = lax.broadcasted_iota(jnp.int32, tiles[0].shape, 1)
    step = count // 2
    while step:
        reach = step * width
        low = (lane // reach) % 2 == 0
        for i in range(count):
            if (i // step) % 2 == 0:
                a, b = tiles[i], tiles[i + step]
                tiles[i] = jnp.where(low, a, pltpu.roll(b, reach, 1))
                tiles[i + step] = jnp.where(low, pltpu.roll(a, LANES - reach, 1), b)
        step //= 2
    return tiles


def arrived_planes(plan, ref, count):
    tiles = plan.tiles
    planes = []
    for f in range(count):
        for c in range(2):
            rows = []
            for p in range(plan.across_y):
                rows.append([ref[p * plan.across_z + q, f, c * tiles : (c + 1) * tiles, :] for q in range(plan.across_z)])
            per_source = [jnp.concatenate([r[q] for r in rows], axis=0) for q in range(plan.across_z)]
            swapped = swap_lanes(per_source, plan.rows_z)
            pieces = []
            for p in range(plan.across_y):
                for g in range(plan.group):
                    pieces.append(swapped[g][p * tiles : (p + 1) * tiles])
            planes.append(jnp.concatenate(pieces, axis=0))
    return planes


def to_waves(plan, ref, count, fore_y, fore_z):
    planes = arrived_planes(plan, ref, count)
    extent = plan.extent
    stacked = jnp.concatenate(
        [jnp.concatenate([planes[2 * f], planes[2 * f + 1]], axis=1) for f in range(count)], axis=0
    )
    along_z = from_right(stacked, fore_z)
    beside = jnp.concatenate(
        [
            jnp.concatenate(
                [along_z[f * extent : (f + 1) * extent, c * LANES : (c + 1) * LANES] for c in range(2)], axis=0
            )
            for f in range(count)
        ],
        axis=1,
    )
    along_y = from_left(fore_y, beside)
    rows = plan.wave_rows
    return [
        [along_y[c * rows : (c + 1) * rows, f * LANES : (f + 1) * LANES] for c in range(2)]
        for f in range(count)
    ]


def send_waves(plan, modes, ref, back_y, back_z):
    count, extent, tiles = len(modes), plan.extent, plan.tiles
    beside = jnp.concatenate([jnp.concatenate(parts, axis=0) for parts in modes], axis=1)
    along_y = from_left(back_y, beside)
    stacked = jnp.concatenate(
        [
            jnp.concatenate(
                [along_y[c * extent : (c + 1) * extent, f * LANES : (f + 1) * LANES] for c in range(2)], axis=1
            )
            for f in range(count)
        ],
        axis=0,
    )
    along_z = from_right(stacked, back_z)
    for f in range(count):
        for c in range(2):
            plane = along_z[f * extent : (f + 1) * extent, c * LANES : (c + 1) * LANES]
            groups = []
            for g in range(plan.group):
                rows = [(p * plan.group + g) * tiles for p in range(plan.across_y)]
                groups.append(jnp.concatenate([plane[r : r + tiles] for r in rows], axis=0))
            swapped = swap_lanes(groups, plan.rows_z)
            for p in range(plan.across_y):
                for q in range(plan.across_z):
                    ref[p * plan.across_z + q, f, c * tiles : (c + 1) * tiles, :] = swapped[q][
                        p * tiles : (p + 1) * tiles
                    ]


def store_first(plan, ref, values, field, count, tile):
    block = 2 * plan.slots * plan.tiles
    for i in range(2 * plan.slots):
        rows = pl.ds(field * block + i * plan.tiles + tile, plan.joint, stride=count * block)
        ref[rows, :] = values[i * plan.joint : (i + 1) * plan.joint]


def load_first(plan, ref, field, count, tile):
    block = 2 * plan.slots * plan.tiles
    return jnp.concatenate(
        [
            ref[pl.ds(field * block + i * plan.tiles + tile, plan.joint, stride=count * block), :]
            for i in range(2 * plan.slots)
        ],
        axis=0,
    )


def begin_kernel(plan, state, fore_high, fore_low, out):
    fore = (fore_high, fore_low)
    count = plan.fields
    for f in range(count):
        values = from_left(fore, state[f], ((1,), (1,)))
        for tile in range(plan.tiles):
            store_first(plan, out, values[:, tile * LANES : (tile + 1) * LANES], f, count, tile)


def product_kernel(plan, arrived, fore_high, fore_low, back_high, back_low, out):
    fore, back = (fore_high, fore_low), (back_high, back_low)
    for pair in range(plan.tiles // 2):
        grid = []
        for f in range(plan.fields):
            lines = jnp.concatenate([load_first(plan, arrived, f, plan.fields, 2 * pair + h) for h in range(2)], axis=1)
            grid.append(from_left(back, lines))
        u, v, w, b = grid
        square_w = w * w
        products = (u * u - square_w, v * v - square_w, u * v, u * w, v * w, u * b, v * b, w * b)
        for f, product in enumerate(products):
            values = from_left(fore, product)
            for h in range(2):
                store_first(plan, out, values[:, h * LANES : (h + 1) * LANES], f, len(products), 2 * pair + h)


def end_kernel(plan, arrived, back_high, back_low, out):
    back = (back_high, back_low)
    for f in range(plan.fields):
        for pair in range(plan.tiles // 2):
            lines = jnp.concatenate([load_first(plan, arrived, f, plan.fields, 2 * pair + h) for h in range(2)], axis=1)
            values = from_left(back, lines)
            for h in range(2):
                start = (2 * pair + h) * LANES
                out[f, start : start + LANES, :] = values[:, h * LANES : (h + 1) * LANES].T


def first_wave(plan, slot):
    place = lax.axis_index("py") * plan.across_z + lax.axis_index("pz")
    return (place + slot * plan.joint).astype(jnp.float32)


def squared(waves):
    return waves[0] * waves[0] + waves[1] * waves[1] + waves[2] * waves[2]


def project(velocity, waves, shrink):
    along = (waves[0] * velocity[0] + waves[1] * velocity[1] + waves[2] * velocity[2]) * shrink
    return [velocity[i] - waves[i] * along for i in range(3)]


def linear(state, waves, square, shrink):
    pushed = project((coriolis * state[1], -coriolis * state[0], state[3]), waves, shrink)
    return [pushed[i] - viscosity * square * state[i] for i in range(3)] + [
        -buoyancy_square * state[2] - diffusivity * square * state[3]
    ]


def propagate(state, waves, square, shrink):
    for half_step in range(2):
        anchor = state
        for order in (4.0, 3.0, 2.0, 1.0):
            change = linear(state, waves, square, shrink)
            state = [a + (0.5 * time_step / order) * g for a, g in zip(anchor, change)]
    return state


def coarse_setup(plan, slot, wave_y, packed_z):
    waves = (first_wave(plan, slot), wave_y[: plan.coarse_rows, :], packed_z[...])
    square = squared(waves)
    keep = (jnp.abs(waves[1]) <= KCO) & (jnp.abs(waves[2]) <= KCO) & (waves[0] <= KCO)
    return waves, square, 1.0 / jnp.maximum(square, 1.0), keep


def pack(plan, parts):
    lane = lax.broadcasted_iota(jnp.int32, (plan.coarse_rows, LANES), 1)
    real, imag = (part[: plan.coarse_rows] for part in parts)
    return jnp.where(lane < LANES // 2, real, pltpu.roll(imag, LANES // 2, 1))


def start_kernel(plan, arrived, fy_h, fy_l, fz_h, fz_l, by_h, by_l, bz_h, bz_l, wave_y, wave_z, start, out):
    modes = to_waves(plan, arrived, plan.fields, (fy_h, fy_l), (fz_h, fz_l))
    waves = (first_wave(plan, pl.program_id(0)), wave_y[...], wave_z[...])
    shrink = 1.0 / jnp.maximum(squared(waves), 1.0)
    parts = [project([modes[i][c] for i in range(3)], waves, shrink) + [modes[3][c]] for c in range(2)]
    modes = [[parts[c][f] for c in range(2)] for f in range(plan.fields)]
    for f in range(plan.fields):
        for c in range(2):
            start[0, f, c] = modes[f][c]
    send_waves(plan, modes, out, (by_h, by_l), (bz_h, bz_l))


def fine_kernel(plan, count, arrived, start, fy_h, fy_l, fz_h, fz_l, wave_y, wave_z, packed_z, fine, local):
    modes = to_waves(plan, arrived, count, (fy_h, fy_l), (fz_h, fz_l))
    slot = pl.program_id(0)
    waves = (first_wave(plan, slot), wave_y[...], wave_z[...])
    kx, ky, kz = waves
    square = squared(waves)
    shrink = 1.0 / jnp.maximum(square, 1.0)
    before = [[start[0, f, c] for c in range(2)] for f in range(plan.fields)]
    after = [[None, None] for _ in range(plan.fields)]
    for c in range(2):
        sign = 1.0 if c == 0 else -1.0
        uu, vv, uv, uw, vw, ub, vb, wb = (sign * modes[i][1 - c] for i in range(count))
        u, v, w, b = (before[f][c] for f in range(plan.fields))
        pushed = project(
            (
                kx * uu + ky * uv + kz * uw + coriolis * v,
                kx * uv + ky * vv + kz * vw - coriolis * u,
                kx * uw + ky * vw + b,
            ),
            waves,
            shrink,
        )
        rates = [pushed[i] - viscosity * square * (u, v, w)[i] for i in range(3)]
        rates.append(kx * ub + ky * vb + kz * wb - buoyancy_square * w - diffusivity * square * b)
        for f in range(plan.fields):
            after[f][c] = before[f][c] + time_step * rates[f]
            fine[0, f, c] = after[f][c]

    @pl.when(slot < plan.coarse_slots)
    def _():
        coarse, square_c, shrink_c, keep = coarse_setup(plan, slot, wave_y, packed_z)
        moved = propagate([pack(plan, parts) for parts in before], coarse, square_c, shrink_c)
        later = lax.axis_index("tm") > 0
        for f in range(plan.fields):
            less = jnp.where(later, moved[f], 0.0)
            local[0, f] = jnp.where(keep, pack(plan, after[f]) - less, 0.0)


def relay_kernel(plan, arrived, local, wave_y, packed_z, carry):
    coarse, square, shrink, keep = coarse_setup(plan, pl.program_id(0), wave_y, packed_z)
    moved = propagate([arrived[0, f] for f in range(plan.fields)], coarse, square, shrink)
    for f in range(plan.fields):
        carry[0, f] = local[0, f] + jnp.where(keep, moved[f], 0.0)


def merge_kernel(plan, arrived, local, fine, by_h, by_l, bz_h, bz_l, wave_y, packed_z, out):
    coarse, square, shrink, keep = coarse_setup(plan, pl.program_id(0), wave_y, packed_z)
    moved = propagate([arrived[0, f] for f in range(plan.fields)], coarse, square, shrink)
    lane = lax.broadcasted_iota(jnp.int32, (plan.coarse_rows, LANES), 1)
    inside = keep & (lane < LANES // 2)
    modes = []
    for f in range(plan.fields):
        carry = local[0, f] + jnp.where(keep, moved[f], 0.0)
        parts = []
        for c in range(2):
            values = fine[0, f, c]
            own = carry if c == 0 else pltpu.roll(carry, LANES // 2, 1)
            upper = jnp.where(inside, own, values[: plan.coarse_rows])
            parts.append(jnp.concatenate([upper, values[plan.coarse_rows :]], axis=0))
        modes.append(parts)
    send_waves(plan, modes, out, (by_h, by_l), (bz_h, bz_l))


def whole(array):
    return pl.BlockSpec(array.shape, lambda *_: (0,) * array.ndim)


def call(body, plan, name, grid, operands, outputs, **cost):
    def spec(shape, block):
        if block is None:
            return pl.BlockSpec(shape, lambda *_: (0,) * len(shape))
        return pl.BlockSpec(*block)

    shapes = [jax.ShapeDtypeStruct(shape, jnp.float32) for shape, _ in outputs]
    return pl.pallas_call(
        functools.partial(body, plan),
        name=name,
        grid=grid,
        in_specs=[spec(array.shape, block) for array, block in operands],
        out_specs=[spec(shape, block) for shape, block in outputs],
        out_shape=shapes,
        compiler_params=pltpu.CompilerParams(vmem_limit_bytes=VMEM_LIMIT),
    )(*[array for array, _ in operands])


def on_device(state_old):
    plan = Plan(state_old.shape, *(lax.axis_size(axis) for axis in ("tm",) + PAIRS))
    fields, joint, slots, tiles = plan.fields, plan.joint, plan.slots, plan.tiles
    products = 8
    block = 2 * slots * tiles

    def flat(count):
        return (joint * count * block, LANES)

    def split_up(array):
        return array.reshape(joint, -1, block, LANES)

    def exchange(array):
        return lax.all_to_all(array, PAIRS, split_axis=0, concat_axis=0, tiled=True)

    fore_first, back_first = (
        [(jnp.asarray(t), None) for t in split_table(table)] for table in plan.first()
    )
    fore_z, back_z = ([(jnp.asarray(t), None) for t in split_table(table)] for table in plan.along_z())
    fore_y, back_y = ([(jnp.asarray(t), None) for t in split_table(table)] for table in plan.along_y())
    wave_y, wave_z, packed_z = ((jnp.asarray(t), None) for t in plan.wave_tables())

    def sent_block(count):
        return ((joint, count, 2 * tiles, LANES), lambda a: (0, 0, a, 0))

    mode_shape = (slots, fields, 2, plan.wave_rows, LANES)
    mode_block = ((1,) + mode_shape[1:], lambda a: (a, 0, 0, 0, 0))
    coarse_shape = (plan.coarse_slots, fields, plan.coarse_rows, LANES)
    last = plan.coarse_slots - 1
    coarse_block = ((1,) + coarse_shape[1:], lambda a: (jnp.minimum(a, last), 0, 0, 0))

    state = state_old.reshape(fields, plan.rows_y * plan.rows_z, plan.extent)
    (sent,) = call(begin_kernel, plan, "begin", (), [(state, None)] + fore_first, [(flat(fields), None)])
    arrived = exchange(split_up(sent))
    start, sent = call(
        start_kernel,
        plan,
        "start",
        (slots,),
        [(arrived, sent_block(fields))] + fore_y + fore_z + back_y + back_z + [wave_y, wave_z],
        [(mode_shape, mode_block), ((joint, fields, block, LANES), sent_block(fields))],
    )
    arrived = exchange(sent).reshape(flat(fields))
    (sent,) = call(
        product_kernel,
        plan,
        "product",
        (),
        [(arrived, None)] + fore_first + back_first,
        [(flat(products), None)],
    )
    arrived = exchange(split_up(sent))
    fine, local = call(
        lambda plan, *refs: fine_kernel(plan, products, *refs),
        plan,
        "fine",
        (slots,),
        [(arrived, sent_block(products)), (start, mode_block)] + fore_y + fore_z + [wave_y, wave_z, packed_z],
        [(mode_shape, mode_block), (coarse_shape, coarse_block)],
    )
    pairs = [(i, i + 1) for i in range(plan.across_t - 1)]
    received = jnp.zeros_like(local)
    carry = local
    for turn in range(plan.across_t - 1):
        received = lax.ppermute(carry, "tm", pairs)
        if turn < plan.across_t - 2:
            (carry,) = call(
                relay_kernel,
                plan,
                "relay",
                (plan.coarse_slots,),
                [(received, coarse_block), (local, coarse_block), wave_y, packed_z],
                [(coarse_shape, coarse_block)],
            )
    (sent,) = call(
        merge_kernel,
        plan,
        "merge",
        (slots,),
        [(received, coarse_block), (local, coarse_block), (fine, mode_block)]
        + back_y
        + back_z
        + [wave_y, packed_z],
        [((joint, fields, block, LANES), sent_block(fields))],
    )
    arrived = exchange(sent).reshape(flat(fields))
    (out,) = call(end_kernel, plan, "end", (), [(arrived, None)] + back_first, [(state.shape, None)])
    return out.reshape(state_old.shape)


def solution(mesh):
    return jax.shard_map(
        on_device,
        mesh=mesh,
        in_specs=(P("tm", None, "py", "pz", None),),
        out_specs=P("tm", None, "py", "pz", None),
        check_vma=False,
    )
```

time: 511 us -> 251 us (0.49); the launches traced: 503 us -> 250 us
  waiting for transfers between devices: 165 us -> 7.5 us
  blocking collectives: 44.3 us -> 201 us
  local copies, waits for them, and re-layouts: 119 us -> 0.67 us
  matrix products: 102 us -> 0 us
  other arithmetic: 49.8 us -> 0 us
  Pallas kernels: 0 us -> 39.7 us
  starting transfers between devices: 20.6 us -> 1.28 us
    all_to_all x1 -> x4, blocking collectives: 44.3 us -> 201 us  [exchange(): return lax.all_to_all(array, PAIRS, split_axis=0, concat_axis=0, tiled=True)]
    all_to_all x3 -> x0, waiting for transfers between devices: 140 us -> none  [the longest x2 80.9 us: to_modes(): lax.all_to_all(spread, ('py', 'pz'), split_axis=3, concat_axis=0, tiled=T...]
    dot_general x12 -> x0, matrix products: 102 us -> none  [product(): jnp.einsum(form, left, right, precision=lax.Precision.HIGHEST, preferred_...]
    unnamed x85 -> x2, local copies, waits for them, and re-layouts: 66.6 us -> 0.67 us
    pallas_call x0 -> x6, Pallas kernels: none -> 39.7 us  [call(): pl.pallas_call(functools.partial(body, plan), name=name, grid=grid, in_sp...]
    all_to_all x4 -> x0, other arithmetic: 26.9 us -> none  [the longest x2 13.9 us: to_grid(): lax.all_to_all(blocks, ('py', 'pz'), split_axis=0, concat_axis=3, tiled=T...]
    all_to_all x3 -> x0, starting transfers between devices: 19.2 us -> none  [the longest x2 13.5 us: to_modes(): lax.all_to_all(spread, ('py', 'pz'), split_axis=3, concat_axis=0, tiled=T...]
    broadcast_in_dim x2 -> x0, local copies, waits for them, and re-layouts: 18.7 us -> none  [to_modes(): spread = product('fyzx,cax->fcayz', physical, fore_first)[None]]
  transfers between devices with their start and end apart: 4 -> 1, of which waited for: 4 -> 1; matrix products, arithmetic and copies ran while one was open for 1% -> 0% of each run, Pallas kernels for 0% -> 0%
where the time goes in v1:
time: 251 us; the launch traced here: 250 us
  blocking collectives  201 us (80%)
  Pallas kernels  39.7 us (16%)
  waiting for transfers between devices  7.5 us (3%)
    all_to_all x4, blocking collectives, exchange(): return lax.all_to_all(array, PAIRS, split_axis=0, concat_axis=0, tiled=True)  201 us
    pallas_call x6, Pallas kernels, call(): pl.pallas_call(functools.partial(body, plan), name=name, grid=grid, in_sp...  39.7 us
    ppermute x1, waiting for transfers between devices, on_device(): received = lax.ppermute(carry, 'tm', pairs)  7.5 us
  transfers between devices with their start and end apart: 1, of which 1 were waited for; matrix products, arithmetic and copies ran while one was open for 0% of the time, Pallas kernels for 0%

profile of v1, /device:TPU:11, one launch (start us, length us, event | category | flops | bytes accessed | tf_op | source)
XLA Modules:
  0.0 250.0 jit_solution(16798215560219638791)
XLA Ops:
  0.0 4.4 %begin.1 = f32[3072,128]{1,0:T(8,128)} custom-call(f32[4,1024,128]{2,1,0:T(8,128)} %bitcast.10, bf16[96,128]{1,0:T(8,128)(2,1)} %constant.30.clone.fore_high, bf16[96,128]{1,0:T(8,128)(2,1)} %constant.31.clone.fore_low), custom_call_target="tpu_custom_call" | custom-call | tf_op jit(solution)/shard_map/begin/pallas_call | solution.py:396
  4.4 43.3 %all_to_all.20.arrived = f32[16,4,48,128]{3,2,1,0:T(8,128)} all-to-all(f32[16,4,48,128]{3,2,1,0:T(8,128)} %bitcast.8), channel_id=1, replica_groups=mesh['tm'=2,'py'=4,'pz'=4] {'py','pz'}, dimensions={0} | all-to-all | bytes 3145728 | tf_op jit(solution)/shard_map/all_to_all | solution.py:420
  47.7 8.9 %start.1 = (f32[3,4,2,88,128]{4,3,2,1,0:T(8,128)}, f32[16,4,48,128]{3,2,1,0:T(8,128)}) custom-call(f32[16,4,48,128]{3,2,1,0:T(8,128)} %all_to_all.20.arrived, bf16[176,256]{1,0:T(8,128)(2,1)} %constant.38.clone.fy_h.refs_2_, bf16[176,256]{1,0:T(8,128)(2,1)} %constant.39.clone.fy_l.refs_3_, bf16[256,256]{1,0:T(8,128)(2,1)} %constant.34.clone.fz_h.refs_4_, ...), custom_call_target="tpu_custom_call" | custom-call | tf_op jit(solution)/shard_map/start/pallas_call | solution.py:396
  56.6 41.1 %all_to_all.21 = f32[16,4,48,128]{3,2,1,0:T(8,128)} all-to-all(f32[16,4,48,128]{3,2,1,0:T(8,128)} %get-tuple-element.9), channel_id=1, replica_groups=mesh['tm'=2,'py'=4,'pz'=4] {'py','pz'}, dimensions={0} | all-to-all | bytes 3145728 | tf_op jit(solution)/shard_map/all_to_all | solution.py:420
  97.7 7.9 %product.1 = f32[6144,128]{1,0:T(8,128)} custom-call(f32[3072,128]{1,0:T(8,128)} %bitcast.9, bf16[96,128]{1,0:T(8,128)(2,1)} %constant.30.clone.fore_high, bf16[96,128]{1,0:T(8,128)(2,1)} %constant.31.clone.fore_low, bf16[128,96]{1,0:T(8,128)(2,1)} %constant.32.clone.back_high, bf16[128,96]{1,0:T(8,128)(2,1)} %constant.33.clone.back_low), custom_call_target="tpu_custom_call" | custom-call | tf_op jit(solution)/shard_map/product/pallas_call | solution.py:396
  105.7 74.8 %all_to_all.22.refs_0_ = f32[16,8,48,128]{3,2,1,0:T(8,128)} all-to-all(f32[16,8,48,128]{3,2,1,0:T(8,128)} %bitcast.6), channel_id=1, replica_groups=mesh['tm'=2,'py'=4,'pz'=4] {'py','pz'}, dimensions={0} | all-to-all | bytes 6291456 | tf_op jit(solution)/shard_map/all_to_all | solution.py:420
  180.5 8.2 %fine.1 = (f32[3,4,2,88,128]{4,3,2,1,0:T(8,128)}, f32[2,4,48,128]{3,2,1,0:T(8,128)}) custom-call(f32[16,8,48,128]{3,2,1,0:T(8,128)} %all_to_all.22.refs_0_, f32[3,4,2,88,128]{4,3,2,1,0:T(8,128)} %get-tuple-element.10.refs_1_, bf16[176,256]{1,0:T(8,128)(2,1)} %constant.38.clone.fy_h.refs_2_, bf16[176,256]{1,0:T(8,128)(2,1)} %constant.39.clone.fy_l.refs_3_, ...), custom_call_target="tpu_custom_call" | custom-call | tf_op jit(solution)/shard_map/fine/pallas_call | solution.py:396
  188.7 1.3 collective-permute-start
  190.0 7.5 %collective-permute-done.arrived = f32[2,4,48,128]{3,2,1,0:T(8,128)S(1)} collective-permute-done((f32[2,4,48,128]{3,2,1,0:T(8,128)}, f32[2,4,48,128]{3,2,1,0:T(8,128)S(1)}, u32[]{:S(2)}, u32[]{:S(2)}) %collective-permute-start) | collective-permute-done | bytes 196640 | tf_op jit(solution)/shard_map/ppermute | solution.py:471
  197.5 0.0 copy-start
  197.5 0.7 copy-done
  198.1 6.0 %merge.1 = f32[16,4,48,128]{3,2,1,0:T(8,128)} custom-call(f32[2,4,48,128]{3,2,1,0:T(8,128)} %copy-done, f32[2,4,48,128]{3,2,1,0:T(8,128)} %get-tuple-element.11.local, f32[3,4,2,88,128]{4,3,2,1,0:T(8,128)} %get-tuple-element.12.fine, bf16[256,176]{1,0:T(8,128)(2,1)} %constant.40.clone.by_h, bf16[256,176]{1,0:T(8,128)(2,1)} %constant.41.clone.by_l, ...), custom_call_target="tpu_custom_call" | custom-call | tf_op jit(solution)/shard_map/merge/pallas_call | solution.py:396
  204.1 41.7 %all_to_all.23 = f32[16,4,48,128]{3,2,1,0:T(8,128)} all-to-all(f32[16,4,48,128]{3,2,1,0:T(8,128)} %merge.1), channel_id=1, replica_groups=mesh['tm'=2,'py'=4,'pz'=4] {'py','pz'}, dimensions={0} | all-to-all | bytes 3145728 | tf_op jit(solution)/shard_map/all_to_all | solution.py:420
  245.8 4.2 %end.1 = f32[4,1024,128]{2,1,0:T(8,128)} custom-call(f32[3072,128]{1,0:T(8,128)} %bitcast.7, bf16[128,96]{1,0:T(8,128)(2,1)} %constant.32.clone.back_high, bf16[128,96]{1,0:T(8,128)(2,1)} %constant.33.clone.back_low), custom_call_target="tpu_custom_call" | custom-call | tf_op jit(solution)/shard_map/end/pallas_call | solution.py:396
Async XLA Ops:
  188.7 8.8 %collective-permute-start = (f32[2,4,48,128]{3,2,1,0:T(8,128)}, f32[2,4,48,128]{3,2,1,0:T(8,128)S(1)}, u32[]{:S(2)}, u32[]{:S(2)}) collective-permute-start(f32[2,4,48,128]{3,2,1,0:T(8,128)} %get-tuple-element.11.local), channel_id=1, source_target_pairs={{0,16},{1,17},{2,18},{3,19},{4,20},{5,21},{6,22},{7,23},{8,24},{9,... | collective-permute-start | bytes 589832 | tf_op jit(solution)/shard_map/ppermute | solution.py:471
  197.5 0.7 copy-start

commit v2 on v1

--- a/solution.py
+++ b/solution.py
@@ -19,7 +19,7 @@
 
 LANES = 128
 PAIRS = ("py", "pz")
-VMEM_LIMIT = 56 * 1024 * 1024
+VMEM_LIMIT = 20 * 1024 * 1024
 
 
 def up_to(value, step):

time: 251 us -> 239 us (0.952)
  Pallas kernels: 39.7 us -> 26.4 us
    pallas_call x6, Pallas kernels: 39.7 us -> 26.4 us  [call(): pl.pallas_call(functools.partial(body, plan), name=name, grid=grid, in_sp...]
where the time goes in v2:
time: 239 us; the launch traced here: 238 us
  blocking collectives  200 us (84%)
  Pallas kernels  26.4 us (11%)
  waiting for transfers between devices  7.29 us (3%)
  local copies, waits for them, and re-layouts  3.15 us (1%)
    all_to_all x4, blocking collectives, exchange(): return lax.all_to_all(array, PAIRS, split_axis=0, concat_axis=0, tiled=True)  200 us
    pallas_call x6, Pallas kernels, call(): pl.pallas_call(functools.partial(body, plan), name=name, grid=grid, in_sp...  26.4 us
    ppermute x1, waiting for transfers between devices, on_device(): received = lax.ppermute(carry, 'tm', pairs)  7.29 us
  transfers between devices with their start and end apart: 1, of which 1 were waited for; matrix products, arithmetic and copies ran while one was open for 0% of the time, Pallas kernels for 0%

profile of v2, /device:TPU:11, one launch (start us, length us, event | category | flops | bytes accessed | tf_op | source)
XLA Modules:
  0.0 238.2 jit_solution(10604500705423318340)
XLA Ops:
  0.0 0.0 copy-start
  0.0 1.6 copy-done
  1.6 0.0 copy-start.14
  1.6 0.7 copy-done.14
  2.3 0.0 copy-start.15
  2.3 0.7 copy-done.15
  3.1 1.7 begin.1
  4.8 0.0 copy-start.1
  4.8 0.0 copy-start.2
  4.8 0.0 copy-start.3
  4.8 0.0 copy-start.4
  4.8 0.0 copy-start.5
  4.8 0.0 copy-start.6
  4.8 0.0 copy-start.7
  4.9 0.0 copy-start.8
  4.9 0.0 copy-start.9
  4.9 0.0 copy-start.10
  4.9 43.1 %all_to_all.20.arrived = f32[16,4,48,128]{3,2,1,0:T(8,128)S(1)} all-to-all(f32[16,4,48,128]{3,2,1,0:T(8,128)S(1)} %bitcast.8), channel_id=1, replica_groups=mesh['tm'=2,'py'=4,'pz'=4] {'py','pz'}, dimensions={0} | all-to-all | bytes 3145728 | tf_op jit(solution)/shard_map/all_to_all | solution.py:420
  48.0 0.0 copy-done.1
  48.0 0.0 copy-done.2
  48.0 0.0 copy-done.3
  48.0 0.0 copy-done.4
  48.0 0.0 copy-done.5
  48.0 0.0 copy-done.6
  48.0 0.0 copy-done.7
  48.0 0.0 copy-done.8
  48.0 0.0 copy-done.9
  48.1 0.0 copy-done.10
  48.1 7.0 %start.1 = (f32[3,4,2,88,128]{4,3,2,1,0:T(8,128)S(1)}, f32[16,4,48,128]{3,2,1,0:T(8,128)S(1)}) custom-call(f32[16,4,48,128]{3,2,1,0:T(8,128)S(1)} %all_to_all.20.arrived, bf16[176,256]{1,0:T(8,128)(2,1)S(1)} %copy-done.9, bf16[176,256]{1,0:T(8,128)(2,1)S(1)} %copy-done.8, bf16[256,256]{1,0:T(8,128)(2,1)S(1)} %copy-done.6, bf16[256,256]{1,0:T(8,128)(2,1)S(1)} %copy-done.5, ...), custom_call_target="tpu_custom_call" | custom-call | tf_op jit(solution)/shard_map/start/pallas_call | solution.py:396
  55.1 0.0 copy-start.11
  55.1 0.0 copy-start.12
  55.1 40.8 %all_to_all.21 = f32[16,4,48,128]{3,2,1,0:T(8,128)S(1)} all-to-all(f32[16,4,48,128]{3,2,1,0:T(8,128)S(1)} %get-tuple-element.9), channel_id=1, replica_groups=mesh['tm'=2,'py'=4,'pz'=4] {'py','pz'}, dimensions={0} | all-to-all | bytes 3145728 | tf_op jit(solution)/shard_map/all_to_all | solution.py:420
  95.9 0.0 copy-done.11
  95.9 0.0 copy-done.12
  95.9 4.9 %product.1 = f32[6144,128]{1,0:T(8,128)S(1)} custom-call(f32[3072,128]{1,0:T(8,128)S(1)} %bitcast.9, bf16[96,128]{1,0:T(8,128)(2,1)S(1)} %copy-done.15, bf16[96,128]{1,0:T(8,128)(2,1)S(1)} %copy-done.14, bf16[128,96]{1,0:T(8,128)(2,1)S(1)} %copy-done.12, bf16[128,96]{1,0:T(8,128)(2,1)S(1)} %copy-done.11), custom_call_target="tpu_custom_call" | custom-call | tf_op jit(solution)/shard_map/product/pallas_call | solution.py:396
  100.8 0.0 copy-start.13
  100.8 74.5 %all_to_all.22.refs_0_ = f32[16,8,48,128]{3,2,1,0:T(8,128)S(1)} all-to-all(f32[16,8,48,128]{3,2,1,0:T(8,128)S(1)} %bitcast.6), channel_id=1, replica_groups=mesh['tm'=2,'py'=4,'pz'=4] {'py','pz'}, dimensions={0} | all-to-all | bytes 6291456 | tf_op jit(solution)/shard_map/all_to_all | solution.py:420
  175.3 0.0 copy-done.13
  175.3 6.2 %fine.1 = (f32[3,4,2,88,128]{4,3,2,1,0:T(8,128)S(1)}, f32[2,4,48,128]{3,2,1,0:T(8,128)S(1)}) custom-call(f32[16,8,48,128]{3,2,1,0:T(8,128)S(1)} %all_to_all.22.refs_0_, f32[3,4,2,88,128]{4,3,2,1,0:T(8,128)S(1)} %get-tuple-element.10.refs_1_, bf16[176,256]{1,0:T(8,128)(2,1)S(1)} %copy-done.9, bf16[176,256]{1,0:T(8,128)(2,1)S(1)} %copy-done.8, ...), custom_call_target="tpu_custom_call" | custom-call | tf_op jit(solution)/shard_map/fine/pallas_call | solution.py:396
  181.5 1.3 collective-permute-start
  182.8 7.3 %collective-permute-done.arrived = f32[2,4,48,128]{3,2,1,0:T(8,128)S(1)} collective-permute-done((f32[2,4,48,128]{3,2,1,0:T(8,128)S(1)}, f32[2,4,48,128]{3,2,1,0:T(8,128)S(1)}, u32[]{:S(2)}, u32[]{:S(2)}) %collective-permute-start) | collective-permute-done | bytes 196640 | tf_op jit(solution)/shard_map/ppermute | solution.py:471
  190.1 3.9 %merge.1 = f32[16,4,48,128]{3,2,1,0:T(8,128)S(1)} custom-call(f32[2,4,48,128]{3,2,1,0:T(8,128)S(1)} %collective-permute-done.arrived, f32[2,4,48,128]{3,2,1,0:T(8,128)S(1)} %get-tuple-element.11.local, f32[3,4,2,88,128]{4,3,2,1,0:T(8,128)S(1)} %get-tuple-element.12.fine, bf16[256,176]{1,0:T(8,128)(2,1)S(1)} %copy-done.2, bf16[256,176]{1,0:T(8,128)(2,1)S(1)} %copy-done.1, ...), custom_call_target="tpu_custom_call" | custom-call | tf_op jit(solution)/shard_map/merge/pallas_call | solution.py:396
  194.0 41.5 %all_to_all.23 = f32[16,4,48,128]{3,2,1,0:T(8,128)S(1)} all-to-all(f32[16,4,48,128]{3,2,1,0:T(8,128)S(1)} %merge.1), channel_id=1, replica_groups=mesh['tm'=2,'py'=4,'pz'=4] {'py','pz'}, dimensions={0} | all-to-all | bytes 3145728 | tf_op jit(solution)/shard_map/all_to_all | solution.py:420
  235.5 2.7 %end.1 = f32[4,1024,128]{2,1,0:T(8,128)} custom-call(f32[3072,128]{1,0:T(8,128)S(1)} %bitcast.7, bf16[128,96]{1,0:T(8,128)(2,1)S(1)} %copy-done.12, bf16[128,96]{1,0:T(8,128)(2,1)S(1)} %copy-done.11), custom_call_target="tpu_custom_call" | custom-call | tf_op jit(solution)/shard_map/end/pallas_call | solution.py:396
Async XLA Ops:
  0.0 1.6 copy-start
  1.6 0.7 copy-start.14
  2.3 0.7 copy-start.15
  4.8 43.2 %copy-start.1 = (bf16[256,176]{1,0:T(8,128)(2,1)S(1)}, bf16[256,176]{1,0:T(8,128)(2,1)}, u32[]{:S(2)}) copy-start(bf16[256,176]{1,0:T(8,128)(2,1)} %constant.41.clone.by_l) | copy-start | bytes 270340
  4.8 43.2 %copy-start.2 = (bf16[256,176]{1,0:T(8,128)(2,1)S(1)}, bf16[256,176]{1,0:T(8,128)(2,1)}, u32[]{:S(2)}) copy-start(bf16[256,176]{1,0:T(8,128)(2,1)} %constant.40.clone.by_h) | copy-start | bytes 270340
  4.8 43.2 %copy-start.3 = (bf16[256,256]{1,0:T(8,128)(2,1)S(1)}, bf16[256,256]{1,0:T(8,128)(2,1)}, u32[]{:S(2)}) copy-start(bf16[256,256]{1,0:T(8,128)(2,1)} %constant.37.clone.bz_l) | copy-start | bytes 393220
  4.8 43.2 %copy-start.4 = (bf16[256,256]{1,0:T(8,128)(2,1)S(1)}, bf16[256,256]{1,0:T(8,128)(2,1)}, u32[]{:S(2)}) copy-start(bf16[256,256]{1,0:T(8,128)(2,1)} %constant.36.clone.bz_h) | copy-start | bytes 393220
  4.8 43.2 %copy-start.5 = (bf16[256,256]{1,0:T(8,128)(2,1)S(1)}, bf16[256,256]{1,0:T(8,128)(2,1)}, u32[]{:S(2)}) copy-start(bf16[256,256]{1,0:T(8,128)(2,1)} %constant.35.clone.fz_l.refs_5_) | copy-start | bytes 393220
  4.8 43.2 %copy-start.6 = (bf16[256,256]{1,0:T(8,128)(2,1)S(1)}, bf16[256,256]{1,0:T(8,128)(2,1)}, u32[]{:S(2)}) copy-start(bf16[256,256]{1,0:T(8,128)(2,1)} %constant.34.clone.fz_h.refs_4_) | copy-start | bytes 393220
  4.8 43.2 %copy-start.7 = (f32[88,128]{1,0:T(8,128)S(1)}, f32[88,128]{1,0:T(8,128)}, u32[]{:S(2)}) copy-start(f32[88,128]{1,0:T(8,128)} %constant.42.clone.wave_y.refs_6_) | copy-start | bytes 135172
  4.9 43.2 %copy-start.8 = (bf16[176,256]{1,0:T(8,128)(2,1)S(1)}, bf16[176,256]{1,0:T(8,128)(2,1)}, u32[]{:S(2)}) copy-start(bf16[176,256]{1,0:T(8,128)(2,1)} %constant.39.clone.fy_l.refs_3_) | copy-start | bytes 270340
  4.9 43.2 %copy-start.9 = (bf16[176,256]{1,0:T(8,128)(2,1)S(1)}, bf16[176,256]{1,0:T(8,128)(2,1)}, u32[]{:S(2)}) copy-start(bf16[176,256]{1,0:T(8,128)(2,1)} %constant.38.clone.fy_h.refs_2_) | copy-start | bytes 270340
  4.9 43.2 %copy-start.10 = (f32[88,128]{1,0:T(8,128)S(1)}, f32[88,128]{1,0:T(8,128)}, u32[]{:S(2)}) copy-start(f32[88,128]{1,0:T(8,128)} %constant.43.clone.wave_z.refs_7_) | copy-start | bytes 135172
  55.1 40.8 %copy-start.11 = (bf16[128,96]{1,0:T(8,128)(2,1)S(1)}, bf16[128,96]{1,0:T(8,128)(2,1)}, u32[]{:S(2)}) copy-start(bf16[128,96]{1,0:T(8,128)(2,1)} %constant.33.clone.back_low) | copy-start | bytes 73732
  55.1 40.8 %copy-start.12 = (bf16[128,96]{1,0:T(8,128)(2,1)S(1)}, bf16[128,96]{1,0:T(8,128)(2,1)}, u32[]{:S(2)}) copy-start(bf16[128,96]{1,0:T(8,128)(2,1)} %constant.32.clone.back_high) | copy-start | bytes 73732
  100.8 74.5 %copy-start.13 = (f32[48,128]{1,0:T(8,128)S(1)}, f32[48,128]{1,0:T(8,128)}, u32[]{:S(2)}) copy-start(f32[48,128]{1,0:T(8,128)} %constant.44.clone.refs_8_.packed_z) | copy-start | bytes 73732
  181.5 8.6 %collective-permute-start = (f32[2,4,48,128]{3,2,1,0:T(8,128)S(1)}, f32[2,4,48,128]{3,2,1,0:T(8,128)S(1)}, u32[]{:S(2)}, u32[]{:S(2)}) collective-permute-start(f32[2,4,48,128]{3,2,1,0:T(8,128)S(1)} %get-tuple-element.11.local), channel_id=1, source_target_pairs={{0,16},{1,17},{2,18},{3,19},{4,20},{5,21},{6,22},{7,23},{8,24},{9,... | collective-permute-start | bytes 589832 | tf_op jit(solution)/shard_map/ppermute | solution.py:471
